TPU v7x, 32 devices: a whole 2x2x4 slice. The times are simulated.
32 devices in a mesh: gz: 8 (over z, x), gy: 4 (over y, core).
Axes of the slice: x: 2, y: 2, z: 4, core: 2. Of those that a mesh axis runs over, the one named last changes fastest.
Arguments:
- source: float32 [32, 64, 512], P('gz', 'gy'), may hold values from -8 to 8
- conduct: float32 [32, 64, 512], P('gz', 'gy'), may hold values from 0.5 to 4
Outputs:
- adjoint: float32 [32, 64, 512], P('gz', 'gy')
- residual: float32 [32, 64, 512], P('gz', 'gy')
All inputs are finite; a program needn't handle non-finite values.
Results may differ from a plain program's by a relative error of at most 0.0003.
Values sent between devices are 32-bit elements; how exact they have to be, the bound alone decides.
A program may use at most 64 MiB of HBM per device.

v0:
```python
import functools

import jax
import jax.numpy as jnp
from jax import lax
from jax.experimental import pallas as pl
from jax.experimental.pallas import tpu as pltpu
from jax.sharding import PartitionSpec as P

DEGREE = 3
COARSE_DEGREE = 4
CYCLES = 2

cheb_low = 0.3
cheb_high = 1.9
heat_step = 4.0
SCALES = (heat_step, heat_step / 4.0, heat_step / 16.0)

HALO = 4
ROWS = 8
MID_REACH = 15
MESH = pl.DeviceIdType.MESH
LANES = 128


def coefficients(steps):
    theta = (cheb_high + cheb_low) / 2.0
    delta = (cheb_high - cheb_low) / 2.0
    sigma = theta / delta
    rho = 1.0 / sigma
    pairs = [(0.0, 1.0 / theta)]
    for _ in range(steps - 1):
        rho_next = 1.0 / (2.0 * sigma - rho)
        pairs.append((rho_next * rho, 2.0 * rho_next / delta))
        rho = rho_next
    return pairs


def window(devices, cells, even):
    reach = -(-MID_REACH // cells)
    count = 2 * reach + 1
    if even:
        count += count % 2
    if count >= devices:
        count = devices
    ahead = count // 2
    return [s if s <= ahead else s - count for s in range(count)]


def select(shape, pick, value):
    rows = lax.broadcasted_iota(jnp.int32, shape, 0)
    columns = lax.broadcasted_iota(jnp.int32, shape, 1)
    return jnp.where(pick(rows, columns), value, 0.0).astype(jnp.bfloat16)


def parts_of(value):
    parts = []
    for _ in range(3):
        parts.append(value.astype(jnp.bfloat16))
        value = value - parts[-1].astype(jnp.float32)
    return parts


def dot(a, b):
    return jnp.dot(a, b, preferred_element_type=jnp.float32)


def pick_rows(lines, value):
    high, middle, low = (dot(lines, part) for part in parts_of(value))
    return high + (middle + low)


def pick_columns(value, columns):
    high, middle, low = (dot(part, columns) for part in parts_of(value))
    return high + (middle + low)


def chunks(value):
    return [value[:, i : i + LANES] for i in range(0, value.shape[1], LANES)]


def join(parts):
    return parts[0] if len(parts) == 1 else jnp.concatenate(parts, axis=1)


def narrow(value):
    parts = chunks(value)
    return join([parts[i] + parts[i + 1] for i in range(0, len(parts), 2)])


def widen(value):
    return join([part for part in chunks(value) for _ in range(2)])


def along_x(here):
    parts = chunks(here)
    lane = lax.broadcasted_iota(jnp.int32, parts[0].shape, 1)
    first = jnp.where(lane == 0, 0.0, pltpu.roll(parts[-1], 1, 1))
    last = jnp.where(lane == LANES - 1, 0.0, pltpu.roll(parts[0], LANES - 1, 1))
    around = [first] + parts + [last]
    return join([around[j] + around[j + 2] for j in range(len(parts))])


def beside_of(w, plane):
    planes = w.shape[0]
    here = w[plane]
    rows = here.shape[0]
    total = w[lax.rem(plane + 1, planes)] + w[lax.rem(plane + planes - 1, planes)]
    total = total + pltpu.roll(here, 1, 0) + pltpu.roll(here, rows - 1, 0)
    return here, total + along_x(here)


def unrolled(count):
    return 4 if count % 4 == 0 else 2 if count % 2 == 0 else 1


def over(planes, own, margin, body):
    if margin is None:
        first, count = 0, planes
    else:
        first, count = planes - margin, own + 2 * margin

    def step(i, carry):
        body(lax.rem(i + first, planes))
        return carry

    lax.fori_loop(0, count, step, 0, unroll=unrolled(count))


class Level:
    def __init__(self, k, inverse, x, d, w, own, scale):
        self.k, self.inverse, self.x, self.d, self.w = k, inverse, x, d, w
        self.own, self.scale, self.planes = own, scale, k.shape[0]

    def run(self, margin, body):
        over(self.planes, self.own, margin, body)

    def prepare(self, margin):
        def body(p):
            self.inverse[p] = 1.0 / (1.0 + 6.0 * self.scale * self.k[p])

        self.run(margin, body)

    def smooth(self, f, steps, margins, zero):
        now = 0
        for step, (keep, gain) in enumerate(coefficients(steps)):
            old, new = self.w[now], self.w[1 - now]

            def body(p, step=step, keep=keep, gain=gain, old=old, new=new):
                if step == 0 and zero:
                    change = gain * (self.inverse[p] * f[p])
                    field = change
                else:
                    here, beside = beside_of(old, p)
                    field = self.x[p]
                    image = field + self.scale * (6.0 * here - beside)
                    change = gain * (self.inverse[p] * (f[p] - image))
                    if step:
                        change = keep * self.d[p] + change
                    field = field + change
                self.d[p] = change
                self.x[p] = field
                new[p] = self.k[p] * field

            self.run(margins[step], body)
            now = 1 - now
        return self.w[now]

    def residual(self, f, x, w, out, margin):
        def body(p):
            here, beside = beside_of(w, p)
            out[p] = f[p] - (x[p] + self.scale * (6.0 * here - beside))

        self.run(margin, body)


def kernel(sizes, z_window, y_window, source, conduct, adjoint, residual,
           src, k0, inv0, x0, d0, wa0, wb0, r0, r1, early, adj, late,
           k1, inv1, x1, d1, wa1, wb1, t1, f1a, f1b,
           k2, inv2, x2, d2, wa2, wb2, f2, halo_send, halo_recv, mid_send, mid_recv):
    gz, gy = sizes
    own_z, own_y, _ = source.shape
    mz, my = own_z // 2, own_y // 2
    me_z, me_y = lax.axis_index("gz"), lax.axis_index("gy")
    at_z = lambda o: (lax.rem(me_z + o + gz, gz), me_y)
    at_y = lambda o: (me_z, lax.rem(me_y + o + gy, gy))

    barrier = pltpu.get_barrier_semaphore()
    greet_z = sorted({o % gz for o in z_window} | {-o % gz for o in z_window})[1:]
    greet_y = sorted({o % gy for o in y_window} | {-o % gy for o in y_window})[1:]
    for o in greet_z:
        pl.semaphore_signal(barrier, inc=1, device_id=at_z(o), device_id_type=MESH)
    for o in greet_y:
        pl.semaphore_signal(barrier, inc=1, device_id=at_y(o), device_id_type=MESH)
    pl.semaphore_wait(barrier, len(greet_z) + len(greet_y))

    started = []

    def send(from_ref, to_ref, send_sem, recv_sem, device):
        copy = pltpu.make_async_remote_copy(
            src_ref=from_ref, dst_ref=to_ref, send_sem=send_sem, recv_sem=recv_sem,
            device_id=device, device_id_type=MESH)
        copy.start()
        started.append(copy)
        return copy

    zs = 3 * own_z
    ys = own_y + 2 * ROWS

    class Halo:
        def __init__(self, number, own, held, depth):
            self.number, self.held, self.depth, self.count = number, held, depth, 0
            self.z = [
                self.put(own.at[pl.ds(own_z - depth, depth)],
                         held.at[pl.ds(zs - depth, depth), pl.ds(0, own_y)], at_z(1)),
                self.put(own.at[pl.ds(0, depth)],
                         held.at[pl.ds(own_z, depth), pl.ds(0, own_y)], at_z(-1)),
            ]
            self.y = self.rows(own, 0, own_z)

        def put(self, from_ref, to_ref, device):
            i = self.count
            self.count += 1
            return send(from_ref, to_ref, halo_send.at[self.number, i],
                        halo_recv.at[self.number, i], device)

        def rows(self, own, first, count):
            planes = pl.ds(first, count)
            return [
                self.put(own.at[planes, pl.ds(own_y - ROWS, ROWS)],
                         self.held.at[planes, pl.ds(own_y + ROWS, ROWS)], at_y(1)),
                self.put(own.at[planes, pl.ds(0, ROWS)],
                         self.held.at[planes, pl.ds(own_y, ROWS)], at_y(-1)),
            ]

        def forward(self):
            self.z[0].wait_recv()
            self.y += self.rows(self.held, zs - self.depth, self.depth)
            self.z[1].wait_recv()
            self.y += self.rows(self.held, own_z, self.depth)

        def wait(self):
            for copy in self.y:
                copy.wait_recv()

    near = sorted(range(len(z_window)), key=lambda s: abs(z_window[s]))
    wide_y = len(y_window)

    class Gather:
        def __init__(self, number, held):
            self.number, self.held = number, held
            self.z = {}
            for s in near[1:][::-1]:
                self.z[s] = send(
                    self.block(0, 0), self.block(s, 0), mid_send.at[number, s * wide_y],
                    mid_recv.at[number, s * wide_y], at_z(-z_window[s]))
            self.y = []
            self.spread(0)

        def block(self, s, t):
            return self.held.at[pl.ds(s * mz, mz), pl.ds(t * my, my)]

        def spread(self, s):
            for t in range(1, wide_y):
                self.y.append(send(
                    self.block(s, 0), self.block(s, t), mid_send.at[self.number, s * wide_y + t],
                    mid_recv.at[self.number, s * wide_y + t], at_y(-y_window[t])))

        def forward(self):
            for s in near[1:]:
                self.z[s].wait_recv()
                self.spread(s)

        def wait(self):
            for copy in self.y:
                copy.wait_recv()

    def coarsen(fine, coarse, planes, rows):
        lines = select((rows // 2, rows), lambda r, c: r == (c >> 1), 0.125)

        def body(p, carry):
            both = fine[2 * p, pl.ds(0, rows)] + fine[2 * p + 1, pl.ds(0, rows)]
            coarse[p, pl.ds(0, rows // 2)] = pick_rows(lines, narrow(both))
            return carry

        lax.fori_loop(0, planes, body, 0, unroll=unrolled(planes))

    fine = Level(k0, inv0, x0, d0, (wa0, wb0), own_z, SCALES[0])
    middle = Level(k1, inv1, x1, d1, (wa1, wb1), None, SCALES[1])
    low = Level(k2, inv2, x2, d2, (wa2, wb2), None, SCALES[2])
    mid_planes, mid_rows, low_planes = k1.shape[0], k1.shape[1], k2.shape[0]

    nx = source.shape[2]
    share = nx // LANES

    def deal(r, c):
        return r == share * (c & (LANES - 1)) + c // LANES

    def own_of(ref):
        return ref.at[pl.ds(0, own_z), pl.ds(0, own_y)]

    def permuted(value, pick):
        columns = select((nx, nx), pick, 1.0)
        flat = value.reshape(own_z * own_y, nx)
        return pick_columns(flat, columns).reshape(own_z, own_y, nx)

    own_of(k0)[...] = permuted(conduct[...], deal)
    conduct_halo = Halo(1, own_of(k0), k0, HALO)
    own_of(src)[...] = permuted(source[...], deal)
    source_halo = Halo(0, own_of(src), src, HALO - 1)
    coarsen(k0, k1, mz, own_y)
    conduct_mid = Gather(0, k1)
    conduct_halo.forward()
    source_halo.forward()
    conduct_halo.wait()
    source_halo.wait()
    fine.prepare(HALO)
    conduct_mid.forward()

    def down(f, f1, number, held, halo_number, depth):
        w = fine.smooth(f, DEGREE, (3, 2, 1), True)
        held[pl.ds(0, own_z), pl.ds(0, own_y)] = x0[pl.ds(0, own_z), pl.ds(0, own_y)]
        fine.residual(f, x0, w, r0, 0)
        coarsen(r0, f1, mz, own_y)
        gather = Gather(number, f1)
        halo = Halo(halo_number, held.at[pl.ds(0, own_z), pl.ds(0, own_y)], held, depth)
        gather.forward()
        return gather, halo

    def solve(f1, halo):
        w = middle.smooth(f1, DEGREE, (None,) * DEGREE, True)
        halo.forward()
        middle.residual(f1, x1, w, t1, None)
        coarsen(t1, f2, low_planes, mid_rows)
        low.smooth(f2, COARSE_DEGREE, (None,) * COARSE_DEGREE, True)
        lines = select((mid_rows, mid_rows // 2), lambda r, c: (r >> 1) == c, 1.0)

        def body(p, carry):
            add = widen(pick_rows(lines, x2[p]))
            for half in range(2):
                field = x1[2 * p + half] + add
                x1[2 * p + half] = field
                wa1[2 * p + half] = k1[2 * p + half] * field
            return carry

        lax.fori_loop(0, low_planes, body, 0, unroll=unrolled(low_planes))
        middle.smooth(f1, DEGREE, (None,) * DEGREE, False)

    def up(f, held, margin):
        def pick(r, c):
            own = (r < own_y + ROWS) & ((r >> 1) == c)
            return own | ((r >= own_y + ROWS) & ((r >> 1) - (ys >> 1) + mid_rows == c))

        lines = select((ys, mid_rows), pick, 1.0)
        pairs = zs // 2
        sides = (margin + 1) // 2

        def body(i, carry):
            pair = lax.rem(i + pairs - sides, pairs)
            late_pair = (pair >= own_z).astype(jnp.int32)
            add = widen(pick_rows(lines, x1[pair + late_pair * (mid_planes - pairs)]))
            for half in range(2):
                p = 2 * pair + half
                field = held[p] + add
                x0[p] = field
                wa0[p] = k0[p] * field
            return carry

        lax.fori_loop(0, mz + 2 * sides, body, 0, unroll=unrolled(mz + 2 * sides))
        return fine.smooth(f, DEGREE, (margin - 1, margin - 2, margin - 3), False)

    gather, halo = down(src, f1a, 1, early, 2, HALO - 1)
    conduct_mid.wait()
    middle.prepare(None)
    coarsen(k1, k2, low_planes, mid_rows)
    low.prepare(None)
    gather.wait()
    solve(f1a, halo)
    halo.wait()
    up(src, early, HALO - 1)
    adj[pl.ds(0, own_z), pl.ds(0, own_y)] = x0[pl.ds(0, own_z), pl.ds(0, own_y)]
    halo = Halo(3, adj.at[pl.ds(0, own_z), pl.ds(0, own_y)], adj, HALO)
    halo.forward()
    halo.wait()

    def weigh(p):
        wa0[p] = k0[p] * adj[p]

    fine.run(HALO, weigh)
    fine.residual(src, adj, wa0, r1, HALO - 1)

    gather, halo = down(r1, f1b, 2, late, 4, HALO)
    gather.wait()
    solve(f1b, halo)
    halo.wait()
    up(r1, late, HALO)

    def finish(p):
        field = adj[p] + x0[p]
        x0[p] = field
        wa0[p] = k0[p] * field

    fine.run(1, finish)
    fine.residual(src, x0, wa0, r0, 0)
    for ref, out in ((x0, adjoint), (r0, residual)):
        out[...] = permuted(own_of(ref)[...], lambda r, c: deal(c, r))
    for copy in started:
        copy.wait_send()


def local(sizes, source, conduct):
    own_z, own_y, nx = source.shape
    z_window = window(sizes[0], own_z // 2, False)
    y_window = window(sizes[1], own_y // 2, True)
    fine = (3 * own_z, own_y + 2 * ROWS, nx)
    mid = (len(z_window) * own_z // 2, len(y_window) * own_y // 2, nx // 2)
    low = tuple(n // 2 for n in mid)
    slots = len(z_window) * len(y_window)
    vmem = lambda shape, count: [pltpu.VMEM(shape, jnp.float32)] * count
    whole = pl.BlockSpec(memory_space=pltpu.VMEM)
    return pl.pallas_call(
        functools.partial(kernel, sizes, z_window, y_window),
        out_shape=[jax.ShapeDtypeStruct(source.shape, jnp.float32)] * 2,
        in_specs=[whole] * 2,
        out_specs=[whole] * 2,
        scratch_shapes=vmem(fine, 12) + vmem(mid, 9) + vmem(low, 7) + [
            pltpu.SemaphoreType.DMA((5, 8)),
            pltpu.SemaphoreType.DMA((5, 8)),
            pltpu.SemaphoreType.DMA((3, slots)),
            pltpu.SemaphoreType.DMA((3, slots)),
        ],
        compiler_params=pltpu.CompilerParams(
            collective_id=0, has_side_effects=True, vmem_limit_bytes=56 * 1024 * 1024
        ),
    )(source, conduct)


def solution(mesh):
    spec = P("gz", "gy", None)
    sizes = (mesh.shape["gz"], mesh.shape["gy"])
    return jax.shard_map(
        functools.partial(local, sizes),
        mesh=mesh,
        in_specs=(spec, spec),
        out_specs=(spec, spec),
        check_vma=False,
    )
```

profile of v0, /device:TPU:1, one launch (start us, length us, event | category | flops | bytes accessed | tf_op | source)
XLA Modules:
  0.0 82.0 jit_solution(1211853198076265573)
XLA Ops:
  0.6 79.0 %shard_map.41 = (f32[4,16,512]{2,1,0:T(8,128)}, f32[4,16,512]{2,1,0:T(8,128)}) custom-call(f32[4,16,512]{2,1,0:T(8,128)} %source.1, f32[4,16,512]{2,1,0:T(8,128)} %conduct.1), custom_call_target="tpu_custom_call" | custom-call | tf_op jit(solution)/shard_map/pallas_call | solution.py:421
  79.7 0.0 copy-start
  79.7 1.6 %copy.6 = f32[4,16,512]{2,1,0:T(8,128)} copy(f32[4,16,512]{2,1,0:T(8,128)} %get-tuple-element.4) | data formatting | bytes 262144
  81.3 0.0 copy-done
  81.3 0.7 copy.7
Async XLA Ops:
  79.7 1.6 %copy-start = (f32[4,16,512]{2,1,0:T(8,128)S(1)}, f32[4,16,512]{2,1,0:T(8,128)}, u32[]{:S(2)}) copy-start(f32[4,16,512]{2,1,0:T(8,128)} %get-tuple-element.5) | copy-start | bytes 393220
where the time goes:
time: 82.1 us; the launch traced here: 82 us
  Pallas kernels  79 us (96%)
  local copies, waits for them, and re-layouts  2.26 us (3%)
    pallas_call x1, Pallas kernels, local(): pl.pallas_call(functools.partial(kernel, sizes, z_window, y_window), out_...  79 us
    unnamed x4, local copies, waits for them, and re-layouts  2.26 us

commit v1 on v0

v1 whole, which is shorter than its diff:
```python
import functools

import jax
import jax.numpy as jnp
from jax import lax
from jax.experimental import pallas as pl
from jax.experimental.pallas import tpu as pltpu
from jax.sharding import PartitionSpec as P

DEGREE = 3
COARSE_DEGREE = 4

cheb_low = 0.3
cheb_high = 1.9
heat_step = 4.0

HALO = 4
PAD = 8
EDGE = 16
MID_REACH = 15
MESH = pl.DeviceIdType.MESH
LANES = 128
TILE = 8


def coefficients(steps):
    theta = (cheb_high + cheb_low) / 2.0
    delta = (cheb_high - cheb_low) / 2.0
    sigma = theta / delta
    rho = 1.0 / sigma
    pairs = [(0.0, 1.0 / theta)]
    for _ in range(steps - 1):
        rho_next = 1.0 / (2.0 * sigma - rho)
        pairs.append((rho_next * rho, 2.0 * rho_next / delta))
        rho = rho_next
    return pairs


def window(devices, reach):
    count = min(2 * reach + 1, devices)
    ahead = count // 2
    return [s if s <= ahead else s - count for s in range(count)]


def parts_of(value, count):
    parts = []
    for _ in range(count):
        parts.append(value.astype(jnp.bfloat16))
        value = value - parts[-1].astype(jnp.float32)
    return parts


def pick_columns(value, columns, count):
    total = None
    for part in reversed(parts_of(value, count)):
        term = jnp.dot(part, columns, preferred_element_type=jnp.float32)
        total = term if total is None else total + term
    return total


def unrolled(count, most):
    return max(u for u in range(1, most + 1) if count % u == 0)


def loop(count, body, most=2):
    def step(i, carry):
        body(i)
        return carry

    lax.fori_loop(0, count, step, 0, unroll=unrolled(count, most))


def rows_at(ref, p, c, row):
    return ref[p, c, pl.ds(row, TILE)]


def beside_of(w, p, row):
    planes, chunks = w.shape[0], w.shape[1]
    after, before = lax.rem(p + 1, planes), lax.rem(p + planes - 1, planes)
    here = [rows_at(w, p, c, row) for c in range(chunks)]
    lane = lax.broadcasted_iota(jnp.int32, here[0].shape, 1)
    first = jnp.where(lane == 0, 0.0, pltpu.roll(here[-1], 1, 1))
    last = jnp.where(lane == LANES - 1, 0.0, pltpu.roll(here[0], LANES - 1, 1))
    around = [first] + here + [last]
    beside = []
    for c in range(chunks):
        total = rows_at(w, after, c, row) + rows_at(w, before, c, row)
        total = total + (rows_at(w, p, c, row - 1) + rows_at(w, p, c, row + 1))
        beside.append(total + (around[c] + around[c + 2]))
    return here, beside


class Level:
    def __init__(self, k, m, g, inverse, d, wa, wb, rows, wraps, most):
        self.k, self.m, self.g, self.inverse, self.d = k, m, g, inverse, d
        self.w = (wa, wb)
        self.rows, self.wraps, self.most = rows, wraps, most

    def run(self, planes, body):
        first, count = planes

        def at(i):
            body(lax.rem(i + first, self.k.shape[0]))

        loop(count, at, self.most)

    def put(self, ref, p, c, row, value):
        ref[p, c, pl.ds(row, TILE)] = value
        if self.wraps:
            if row == self.rows[0]:
                ref[p, c, pl.ds(self.rows[-1] + TILE, 1)] = value[:1]
            if row == self.rows[-1]:
                ref[p, c, pl.ds(self.rows[0] - 1, 1)] = value[TILE - 1 :]

    def wrap(self, ref):
        def body(p):
            for c in range(ref.shape[1]):
                end = self.rows[-1] + TILE
                ref[p, c, pl.ds(end, 1)] = ref[p, c, pl.ds(self.rows[0], 1)]
                ref[p, c, pl.ds(self.rows[0] - 1, 1)] = ref[p, c, pl.ds(end - 1, 1)]

        loop(ref.shape[0], body, 4)

    def second(self, u, new, planes, steps):
        start = coefficients(steps)[0][1]
        keep, gain = coefficients(steps)[1]
        mine, theirs = keep * start + gain * (1.0 - start), gain * start

        def body(p):
            for row in self.rows:
                here, beside = beside_of(u, p, row)
                for c in range(len(here)):
                    change = mine * here[c] + theirs * (rows_at(self.m, p, c, row) * beside[c])
                    self.d[p, c, pl.ds(row, TILE)] = change
                    self.put(new, p, c, row, start * here[c] + change)

        self.run(planes, body)

    def step(self, u, old, new, planes, pair, save=True, plus=None):
        keep, gain = pair

        def body(p):
            for row in self.rows:
                here, beside = beside_of(old, p, row)
                for c in range(len(here)):
                    pull = rows_at(self.m, p, c, row) * beside[c] + rows_at(u, p, c, row)
                    change = gain * (pull - here[c])
                    if keep:
                        change = keep * rows_at(self.d, p, c, row) + change
                    if save:
                        self.d[p, c, pl.ds(row, TILE)] = change
                    value = here[c] + change
                    if plus is not None:
                        value = value + rows_at(plus, p, c, row)
                    self.put(new, p, c, row, value)

        self.run(planes, body)

    def residual(self, u, w, out, planes, rows):
        def body(p):
            for row in rows:
                here, beside = beside_of(w, p, row)
                for c in range(len(here)):
                    pull = (rows_at(u, p, c, row) - here[c]) * rows_at(self.g, p, c, row)
                    out[p, c, pl.ds(row, TILE)] = pull + beside[c]

        self.run(planes, body)


def coarsen(fine, coarse, planes, rows, factor, m=None):
    def body(p):
        for c in range(coarse.shape[1]):
            for row in range(0, rows, TILE):
                total = None
                for half in range(2):
                    for chunk in (2 * c, 2 * c + 1):
                        for odd in range(2):
                            at = pl.ds(PAD + 2 * row + odd, TILE, stride=2)
                            term = fine[2 * p + half, chunk, at]
                            total = term if total is None else total + term
                total = total * factor
                if m is not None:
                    total = total * rows_at(m, p, c, PAD + row)
                coarse[p, c, pl.ds(PAD + row, TILE)] = total

    loop(planes, body, 2)


def kernel(sizes, z_window, pairs, source, conduct, adjoint, residual,
           raw_f, raw_k, f0, k0, m0, g0, inv0, u0a, u0b, wa0, wb0, d0, ha, hb, ws, t0,
           k1, m1, g1, inv1, u1a, u1b, wa1, wb1, d1, t1, e0,
           k2, m2, g2, inv2, u2, wa2, wb2, d2, e1,
           load_sem, send_sem, recv_sem):
    gz, gy = sizes
    own_z, own_y, nx = source.shape
    mz, my = own_z // 2, own_y // 2
    zs = k0.shape[0]
    mid_planes, low_planes = k1.shape[0], k2.shape[0]
    mid_rows, low_rows = k1.shape[2] - 2 * PAD, k2.shape[2] - 2 * PAD
    me_z, me_y = lax.axis_index("gz"), lax.axis_index("gy")
    core = lax.rem(me_y, 2)
    mate = 1 - 2 * core
    slots = 2 * len(pairs)

    def at(oz, oy):
        return (lax.rem(me_z + oz + gz, gz), lax.rem(me_y + oy + gy, gy))

    load_k = pltpu.make_async_copy(conduct, raw_k, load_sem.at[0])
    load_f = pltpu.make_async_copy(source, raw_f, load_sem.at[1])
    load_k.start()
    load_f.start()

    barrier = pltpu.get_barrier_semaphore()
    near = [-1, 0, 1]
    greet = {(oz % gz, oy % gy) for oz in near for oy in near}
    for s in z_window:
        greet |= {(s % gz, 0), (-s % gz, 0)}
    for s in pairs:
        greet |= {(0, 2 * s % gy), (0, -2 * s % gy)}
    greet = sorted(greet - {(0, 0)})
    for oz, oy in greet:
        pl.semaphore_signal(barrier, inc=1, device_id=at(oz, oy), device_id_type=MESH)

    share = nx // LANES

    def deal(r, c, value):
        pick = r == share * (c & (LANES - 1)) + c // LANES
        return jnp.where(pick, value, 0.0).astype(jnp.bfloat16)

    rows = lax.broadcasted_iota(jnp.int32, (nx, nx), 0)
    columns = lax.broadcasted_iota(jnp.int32, (nx, nx), 1)

    def enter(raw, out, row, value):
        flat = pick_columns(raw[...].reshape(own_z * own_y, nx), deal(rows, columns, value), 3)
        for p in range(own_z):
            for c in range(share):
                piece = flat[p * own_y : (p + 1) * own_y, c * LANES : (c + 1) * LANES]
                out[p, c, pl.ds(row, own_y)] = piece

    own_tiles = tuple(range(PAD, PAD + own_y, TILE))
    fine_tiles = tuple(range(PAD - HALO, PAD + own_y + HALO, TILE))
    fine = Level(k0, m0, g0, inv0, d0, wa0, wb0, fine_tiles, False, 2)
    mid = Level(k1, m1, g1, inv1, d1, wa1, wb1, tuple(range(PAD, PAD + mid_rows, TILE)), True, 2)
    low = Level(k2, m2, g2, inv2, d2, wa2, wb2, tuple(range(PAD, PAD + low_rows, TILE)), True, 8)

    def around(margin):
        return (zs - margin, own_z + 2 * margin)

    def weigh(level, p, row, whole=True):
        for c in range(level.k.shape[1]):
            inverse = 1.0 / rows_at(level.k, p, c, row)
            g = 6.0 + inverse
            level.m[p, c, pl.ds(row, TILE)] = 1.0 / g
            if whole:
                level.g[p, c, pl.ds(row, TILE)] = g
                level.inverse[p, c, pl.ds(row, TILE)] = inverse

    load_k.wait()
    enter(raw_k, k0, PAD, heat_step)

    def own_weights(p):
        for row in own_tiles:
            weigh(fine, p, row)

    loop(own_z, own_weights)
    load_f.wait()
    enter(raw_f, f0, 0, 1.0)

    def own_start(p):
        for c in range(share):
            for row in own_tiles:
                value = rows_at(m0, p, c, row) * rows_at(f0, p, c, row - PAD)
                u0a[p, c, pl.ds(row, TILE)] = value

    loop(own_z, own_start)
    coarsen(k0, k1, mz, my, 0.125 / 4.0)

    def own_mid_weights(p):
        for row in range(PAD, PAD + my, TILE):
            weigh(mid, p, row)

    loop(mz, own_mid_weights)

    pl.semaphore_wait(barrier, len(greet))

    counts = {"send": 0, "recv": 0}
    unsent = []

    def take(kind):
        counts[kind] += 1
        sems = send_sem if kind == "send" else recv_sem
        return sems.at[counts[kind] - 1]

    def copy_of(from_ref, to_ref, sent, got, device):
        return pltpu.make_async_remote_copy(
            src_ref=from_ref, dst_ref=to_ref, send_sem=sent, recv_sem=got,
            device_id=device, device_id_type=MESH)

    def send(from_ref, to_ref, device):
        copy = copy_of(from_ref, to_ref, take("send"), take("recv"), device)
        copy.start()
        unsent.append(copy)
        return copy

    odd = lax.rem(me_z, 2)
    sides = [2 * odd - 1, 1 - 2 * odd]

    def face(own, held, side, skip, depth, row_side, depth_y, device):
        up = side > 0
        count = depth - skip
        start = jnp.where(up, own_z - depth, skip)
        land = jnp.where(up, zs - depth, own_z + skip)
        if row_side == 0:
            row, to_row, height = PAD, PAD, own_y
        elif row_side > 0:
            row, to_row, height = PAD + own_y - depth_y, PAD - depth_y, depth_y
        else:
            row, to_row, height = PAD, PAD + own_y, depth_y
        return send(own.at[pl.ds(start, count), :, pl.ds(row, height)],
                    held.at[pl.ds(land, count), :, pl.ds(to_row, height)], device)

    def flank(own, held, row_side, depth_y):
        planes = pl.ds(0, own_z)
        if row_side > 0:
            row, to_row = PAD + own_y - depth_y, PAD - depth_y
        else:
            row, to_row = PAD, PAD + own_y
        return send(own.at[planes, :, pl.ds(row, depth_y)],
                    held.at[planes, :, pl.ds(to_row, depth_y)], at(0, row_side))

    def surround(jobs):
        copies = []
        for number, side in enumerate(sides):
            for ref, depth, depth_y, corner, corner_y in jobs:
                copies.append(face(ref, ref, side, 0, depth, 0, 0, at(side, 0)))
            for ref, depth, depth_y, corner, corner_y in jobs:
                for row_side in (1, -1):
                    copies.append(face(ref, ref, side, 0, corner, row_side, corner_y,
                                       at(side, row_side)))
            if number == 0:
                for ref, depth, depth_y, corner, corner_y in jobs:
                    for row_side in (1, -1):
                        copies.append(flank(ref, ref, row_side, depth_y))
        return copies

    def beyond(ref):
        copies = []
        for side in sides:
            copies.append(face(ref, ref, side, 2, HALO, 0, 0, at(side, 0)))
            for row_side in (1, -1):
                copies.append(face(ref, ref, side, 2, HALO - 1, row_side, 1, at(side, row_side)))
        return copies

    def await_all(copies):
        for copy in copies:
            copy.wait_recv()

    far_first = sorted(range(len(z_window)), key=lambda s: -abs(z_window[s]))[:-1]

    class Gather:
        def __init__(self, held):
            self.held = held
            self.z = {}
            for s in far_first:
                self.z[s] = send(self.block(0, 0), self.block(s, 0), at(-z_window[s], 0))
            self.y = {n: (take("send"), take("recv")) for n in range(1, len(pairs))}
            self.spread(0)

        def rows(self, slot):
            return pl.ds(pl.multiple_of(PAD + slot * my, TILE), my)

        def block(self, s, slot):
            return self.held.at[pl.ds(s * mz, mz), :, self.rows(slot)]

        def column(self, slot):
            return self.held.at[:, :, self.rows(slot)]

        def spread(self, s):
            for n in range(1, len(pairs)):
                slot = 2 * pairs[n] % slots
                sent, got = self.y[n]
                copy_of(self.block(s, 0), self.block(s, slot), sent, got,
                        at(0, -2 * pairs[n])).start()

        def mirror(self, n):
            slot = 2 * pairs[n] % slots
            to_slot = lax.rem(slot - mate + slots, slots)
            return send(self.column(slot), self.column(to_slot), at(0, mate))

        def forward(self):
            for s in far_first:
                self.z[s].wait_recv()
                self.spread(s)
            self.mate = [self.mirror(0)]

        def across(self):
            for n in range(1, len(pairs)):
                slot = 2 * pairs[n] % slots
                whole = copy_of(self.column(0), self.column(slot), *self.y[n],
                                at(0, -2 * pairs[n]))
                whole.wait_recv()
                unsent.append(whole)
                self.mate.append(self.mirror(n))

        def wait(self):
            await_all(self.mate)

    first = surround([(u0a, 3, 3, 2, 2), (k0, 2, HALO, 2, 3)])
    gather_k = Gather(k1)
    await_all(first)

    steps = coefficients(DEGREE)

    def weights(p):
        for row in fine_tiles:
            weigh(fine, p, row, False)

    def some_weights(start, count):
        loop(count, lambda i: weights(lax.rem(i + start, zs)))

    some_weights(0, own_z + 2)
    some_weights(zs - 2, 2)

    def down(u, held, u1, between=None):
        fine.second(u, wa0, around(2), DEGREE)
        if between:
            between()
        fine.step(u, wa0, wb0, around(1), steps[2], save=False)
        fine.residual(u, wb0, t0, (0, own_z), own_tiles)
        coarsen(t0, u1, mz, my, 0.125, m1)
        gather = Gather(u1)

        def hold(p):
            for c in range(share):
                for row in own_tiles:
                    held[p, c, pl.ds(row, TILE)] = rows_at(wb0, p, c, row)

        loop(own_z, hold)
        return gather

    def solve(u1):
        everywhere = (0, mid_planes)
        mid.wrap(u1)
        mid.second(u1, wa1, everywhere, DEGREE)
        mid.step(u1, wa1, wb1, everywhere, steps[2], save=False)
        mid.residual(u1, wb1, t1, everywhere, mid.rows)
        coarsen(t1, u2, low_planes, low_rows, 0.125, m2)
        low.wrap(u2)
        low_steps = coefficients(COARSE_DEGREE)
        deep = (0, low_planes)
        low.second(u2, wa2, deep, COARSE_DEGREE)
        low.step(u2, wa2, wb2, deep, low_steps[2])
        low.step(u2, wb2, wa2, deep, low_steps[3], save=False)
        margin = HALO // 2 + DEGREE
        pairs_first, pairs_count = -(-margin // 2), mz // 2 + 2 * -(-margin // 2)
        pairs_count = min(pairs_count, low_planes)

        def lift(i):
            p = lax.rem(i + low_planes - pairs_first, low_planes)
            for row in low.rows:
                value = rows_at(wa2, p, 0, row) * rows_at(inv2, p, 0, row)
                spot = PAD + 2 * (row - PAD)
                for o in range(2):
                    e1[p, 0, pl.ds(spot + o, TILE, stride=2)] = value

        loop(pairs_count, lift)

        def add(i):
            p = lax.rem(i + low_planes - pairs_first, low_planes)
            for half in range(2):
                q = 2 * p + half
                for c in range(k1.shape[1]):
                    for row in mid.rows:
                        value = rows_at(wb1, q, c, row)
                        value = value + rows_at(k1, q, c, row) * rows_at(e1, p, c // 2, row)
                        mid.put(wb1, q, c, row, value)

        loop(pairs_count, add, 1)

        def near_own(reach):
            if mz + 2 * reach >= mid_planes:
                return everywhere
            return (mid_planes - reach, mz + 2 * reach)

        reach = HALO // 2
        mid.step(u1, wb1, wa1, near_own(reach + 2), steps[0])
        mid.step(u1, wa1, wb1, near_own(reach + 1), steps[1])
        mid.step(u1, wb1, wa1, near_own(reach), steps[2], save=False)

        def lift_fine(i):
            q = lax.rem(i + mid_planes - reach, mid_planes)
            for c in range(k1.shape[1]):
                for row in range(-TILE, my + TILE, TILE):
                    here = PAD + row % mid_rows
                    value = rows_at(wa1, q, c, here) * rows_at(inv1, q, c, here)
                    for o in range(2):
                        e0[i, c, pl.ds(EDGE + 2 * row + o, TILE, stride=2)] = value

        loop(mz + 2 * reach, lift_fine)

    def up(u, held, out, plus=None):
        reach = HALO // 2

        def body(i):
            for half in range(2):
                p = lax.rem(2 * i + half + zs - HALO, zs)
                for c in range(share):
                    for row in fine_tiles:
                        add = rows_at(e0, i, c // 2, EDGE + row - PAD)
                        value = rows_at(held, p, c, row) + rows_at(k0, p, c, row) * add
                        wa0[p, c, pl.ds(row, TILE)] = value

        loop(mz + 2 * reach, body, 1)
        fine.step(u, wa0, wb0, around(3), steps[0])
        fine.step(u, wb0, wa0, around(2), steps[1])
        fine.step(u, wa0, out, around(1), steps[2], save=False, plus=plus)

    def remain(p, row, w):
        here, beside = beside_of(w, p, row)
        values = []
        for c in range(share):
            pull = rows_at(f0, p, c, row - PAD) - rows_at(g0, p, c, row) * here[c]
            values.append(pull + beside[c])
        return here, values

    gather = down(u0a, ha, u1a, gather_k.forward)
    gather_k.across()
    more = beyond(k0)
    gather.forward()
    held = surround([(ha, HALO, HALO, 3, 3)])
    gather_k.wait()

    def mid_weights(p):
        for row in mid.rows:
            weigh(mid, p, row)

    loop(mid_planes, mid_weights)
    coarsen(k1, k2, low_planes, low_rows, 0.125 / 4.0)

    def low_weights(p):
        for row in low.rows:
            weigh(low, p, row)

    loop(low_planes, low_weights, 4)
    gather.across()
    gather.wait()
    solve(u1a)
    await_all(more)
    some_weights(own_z + 2, 1)
    some_weights(zs - 3, 1)
    await_all(held)
    up(u0a, ha, ws)

    def again(p):
        for row in own_tiles:
            _, values = remain(p, row, ws)
            for c in range(share):
                u0b[p, c, pl.ds(row, TILE)] = rows_at(m0, p, c, row) * values[c]

    loop(own_z, again)
    second = surround([(u0b, 3, 3, 2, 2)])
    await_all(second)
    gather = down(u0b, hb, u1b)
    gather.forward()
    held = surround([(hb, HALO, HALO, 3, 3)])
    gather.across()
    gather.wait()
    solve(u1b)
    await_all(held)
    up(u0b, hb, wb0, plus=ws)

    back = deal(columns, rows, 1.0)

    def leave(pieces, out):
        flat = jnp.concatenate(pieces, axis=1)
        out[...] = pick_columns(flat, back, 2).reshape(own_z, own_y, nx)

    def finish(p):
        for row in own_tiles:
            _, values = remain(p, row, wb0)
            for c in range(share):
                t0[p, c, pl.ds(row, TILE)] = values[c]

    loop(own_z, finish)

    def pieces_of(ref, weight=None):
        pieces = []
        for c in range(share):
            parts = []
            for p in range(own_z):
                value = ref[p, c, pl.ds(PAD, own_y)]
                if weight is not None:
                    value = value * weight[p, c, pl.ds(PAD, own_y)]
                parts.append(value)
            pieces.append(jnp.concatenate(parts, axis=0))
        return pieces

    leave(pieces_of(wb0, inv0), adjoint)
    leave(pieces_of(t0), residual)
    for copy in unsent:
        copy.wait_send()
    assert counts["send"] <= send_sem.shape[0] and counts["recv"] <= recv_sem.shape[0], counts


def local(sizes, source, conduct):
    own_z, own_y, nx = source.shape
    z_window = window(sizes[0], -(-MID_REACH // (own_z // 2)))
    pairs = window(sizes[1] // 2, -(-MID_REACH // own_y))
    chunks = nx // LANES
    mz, my = own_z // 2, own_y // 2
    mid_planes, mid_rows = len(z_window) * mz, 2 * len(pairs) * my
    fine = (own_z + 2 * HALO, chunks, own_y + 2 * PAD, LANES)
    mid = (mid_planes, chunks // 2, mid_rows + 2 * PAD, LANES)
    low = (mid_planes // 2, chunks // 4, mid_rows // 2 + 2 * PAD, LANES)
    lifted = (mz + HALO, chunks // 2, own_y + 2 * EDGE, LANES)
    lifted_low = (mid_planes // 2, chunks // 4, mid_rows + 2 * PAD, LANES)
    inside = (own_z, chunks, own_y, LANES)
    vmem = lambda shape, count: [pltpu.VMEM(shape, jnp.float32)] * count
    gathers = 3 * (len(z_window) - 1 + 2 * len(pairs) - 1)
    copies = 5 * 8 + 6 + gathers
    return pl.pallas_call(
        functools.partial(kernel, sizes, z_window, pairs),
        out_shape=[pltpu.VMEM(source.shape, jnp.float32)] * 2,
        in_specs=[pl.BlockSpec(memory_space=pl.ANY)] * 2,
        out_specs=[pl.BlockSpec(memory_space=pltpu.VMEM)] * 2,
        scratch_shapes=vmem(source.shape, 2) + vmem(inside, 1) + vmem(fine, 13)
        + vmem(mid, 10) + vmem(lifted, 1) + vmem(low, 8) + vmem(lifted_low, 1) + [
            pltpu.SemaphoreType.DMA((2,)),
            pltpu.SemaphoreType.DMA((copies,)),
            pltpu.SemaphoreType.DMA((copies,)),
        ],
        compiler_params=pltpu.CompilerParams(
            collective_id=0, has_side_effects=True, vmem_limit_bytes=56 * 1024 * 1024
        ),
    )(source, conduct)


def solution(mesh):
    spec = P("gz", "gy", None)
    sizes = (mesh.shape["gz"], mesh.shape["gy"])
    return jax.shard_map(
        functools.partial(local, sizes),
        mesh=mesh,
        in_specs=(spec, spec),
        out_specs=(spec, spec),
        check_vma=False,
    )
```

time: 82.1 us -> 63.2 us (0.77)
  Pallas kernels: 79 us -> 61.2 us
  local copies, waits for them, and re-layouts: 2.26 us -> 1.31 us
    pallas_call x1, Pallas kernels: 79 us -> 61.2 us  [local(): pl.pallas_call(functools.partial(kernel, sizes, z_window, pairs), out_sha...]
    unnamed x4 -> x2, local copies, waits for them, and re-layouts: 2.26 us -> 1.31 us
where the time goes in v1:
time: 63.2 us; the launch traced here: 63.1 us
  Pallas kernels  61.2 us (97%)
  local copies, waits for them, and re-layouts  1.31 us (2%)
  between operations  0.64 us (1%)
    pallas_call x1, Pallas kernels, local(): pl.pallas_call(functools.partial(kernel, sizes, z_window, pairs), out_sha...  61.2 us
    unnamed x2, local copies, waits for them, and re-layouts  1.31 us

profile of v1, /device:TPU:1, one launch (start us, length us, event | category | flops | bytes accessed | tf_op | source)
XLA Modules:
  0.0 63.1 jit_solution(15867783813513580603)
XLA Ops:
  0.6 61.2 %shard_map.41 = (f32[4,16,512]{2,1,0:T(8,128)S(1)}, f32[4,16,512]{2,1,0:T(8,128)S(1)}) custom-call(f32[4,16,512]{2,1,0:T(8,128)} %source.1, f32[4,16,512]{2,1,0:T(8,128)} %conduct.1), custom_call_target="tpu_custom_call" | custom-call | tf_op jit(solution)/shard_map/pallas_call | solution.py:621
  61.8 0.7 %copy.6 = f32[4,16,512]{2,1,0:T(8,128)} copy(f32[4,16,512]{2,1,0:T(8,128)S(1)} %get-tuple-element.2) | data formatting | bytes 262144
  62.5 0.7 %copy.7 = f32[4,16,512]{2,1,0:T(8,128)} copy(f32[4,16,512]{2,1,0:T(8,128)S(1)} %get-tuple-element.3) | data formatting | bytes 262144

commit v2 on v1

--- a/solution.py
+++ b/solution.py
@@ -62,7 +62,7 @@
     return max(u for u in range(1, most + 1) if count % u == 0)
 
 
-def loop(count, body, most=2):
+def loop(count, body, most=16):
     def step(i, carry):
         body(i)
         return carry
@@ -91,10 +91,10 @@
 
 
 class Level:
-    def __init__(self, k, m, g, inverse, d, wa, wb, rows, wraps, most):
+    def __init__(self, k, m, g, inverse, d, wa, wb, rows, wraps):
         self.k, self.m, self.g, self.inverse, self.d = k, m, g, inverse, d
         self.w = (wa, wb)
-        self.rows, self.wraps, self.most = rows, wraps, most
+        self.rows, self.wraps = rows, wraps
 
     def run(self, planes, body):
         first, count = planes
@@ -102,7 +102,7 @@
         def at(i):
             body(lax.rem(i + first, self.k.shape[0]))
 
-        loop(count, at, self.most)
+        loop(count, at)
 
     def put(self, ref, p, c, row, value):
         ref[p, c, pl.ds(row, TILE)] = value
@@ -119,7 +119,7 @@
                 ref[p, c, pl.ds(end, 1)] = ref[p, c, pl.ds(self.rows[0], 1)]
                 ref[p, c, pl.ds(self.rows[0] - 1, 1)] = ref[p, c, pl.ds(end - 1, 1)]
 
-        loop(ref.shape[0], body, 4)
+        loop(ref.shape[0], body)
 
     def second(self, u, new, planes, steps):
         start = coefficients(steps)[0][1]
@@ -183,7 +183,7 @@
                     total = total * rows_at(m, p, c, PAD + row)
                 coarse[p, c, pl.ds(PAD + row, TILE)] = total
 
-    loop(planes, body, 2)
+    loop(planes, body)
 
 
 def kernel(sizes, z_window, pairs, source, conduct, adjoint, residual,
@@ -239,9 +239,9 @@
 
     own_tiles = tuple(range(PAD, PAD + own_y, TILE))
     fine_tiles = tuple(range(PAD - HALO, PAD + own_y + HALO, TILE))
-    fine = Level(k0, m0, g0, inv0, d0, wa0, wb0, fine_tiles, False, 2)
-    mid = Level(k1, m1, g1, inv1, d1, wa1, wb1, tuple(range(PAD, PAD + mid_rows, TILE)), True, 2)
-    low = Level(k2, m2, g2, inv2, d2, wa2, wb2, tuple(range(PAD, PAD + low_rows, TILE)), True, 8)
+    fine = Level(k0, m0, g0, inv0, d0, wa0, wb0, fine_tiles, False)
+    mid = Level(k1, m1, g1, inv1, d1, wa1, wb1, tuple(range(PAD, PAD + mid_rows, TILE)), True)
+    low = Level(k2, m2, g2, inv2, d2, wa2, wb2, tuple(range(PAD, PAD + low_rows, TILE)), True)
 
     def around(margin):
         return (zs - margin, own_z + 2 * margin)
@@ -319,37 +319,45 @@
         return send(own.at[pl.ds(start, count), :, pl.ds(row, height)],
                     held.at[pl.ds(land, count), :, pl.ds(to_row, height)], device)
 
-    def flank(own, held, row_side, depth_y):
-        planes = pl.ds(0, own_z)
+    def flank(own, held, row_side, skip, depth_y):
+        planes, height = pl.ds(0, own_z), depth_y - skip
         if row_side > 0:
             row, to_row = PAD + own_y - depth_y, PAD - depth_y
         else:
-            row, to_row = PAD, PAD + own_y
-        return send(own.at[planes, :, pl.ds(row, depth_y)],
-                    held.at[planes, :, pl.ds(to_row, depth_y)], at(0, row_side))
+            row, to_row = PAD + skip, PAD + own_y + skip
+        return send(own.at[planes, :, pl.ds(row, height)],
+                    held.at[planes, :, pl.ds(to_row, height)], at(0, row_side))
 
     def surround(jobs):
         copies = []
         for number, side in enumerate(sides):
-            for ref, depth, depth_y, corner, corner_y in jobs:
-                copies.append(face(ref, ref, side, 0, depth, 0, 0, at(side, 0)))
-            for ref, depth, depth_y, corner, corner_y in jobs:
+            for ref, skip, depth, depth_y, corners in jobs:
+                copies.append(face(ref, ref, side, skip, depth, 0, 0, at(side, 0)))
+            for ref, skip, depth, depth_y, corners in jobs:
                 for row_side in (1, -1):
-                    copies.append(face(ref, ref, side, 0, corner, row_side, corner_y,
-                                       at(side, row_side)))
+                    for n, corner in enumerate(corners):
+                        copies.append(face(ref, ref, side, n, n + 1, row_side, corner,
+                                           at(side, row_side)))
             if number == 0:
-                for ref, depth, depth_y, corner, corner_y in jobs:
+                for ref, skip, depth, depth_y, corners in jobs:
                     for row_side in (1, -1):
-                        copies.append(flank(ref, ref, row_side, depth_y))
+                        copies.append(flank(ref, ref, row_side, skip, depth_y))
         return copies
 
     def beyond(ref):
-        copies = []
+        copies = [face(ref, ref, sides[1], 2, HALO, 0, 0, at(sides[1], 0))]
         for side in sides:
-            copies.append(face(ref, ref, side, 2, HALO, 0, 0, at(side, 0)))
             for row_side in (1, -1):
                 copies.append(face(ref, ref, side, 2, HALO - 1, row_side, 1, at(side, row_side)))
         return copies
+
+    def relay(ref):
+        up = sides[1] > 0
+        start = jnp.where(up, own_z, zs - 2)
+        land = jnp.where(up, zs - HALO, own_z + 2)
+        own_rows = pl.ds(PAD, own_y)
+        return [send(ref.at[pl.ds(start, 2), :, own_rows], ref.at[pl.ds(land, 2), :, own_rows],
+                     at(2 * sides[1], 0))]
 
     def await_all(copies):
         for copy in copies:
@@ -405,9 +413,11 @@
         def wait(self):
             await_all(self.mate)
 
-    first = surround([(u0a, 3, 3, 2, 2), (k0, 2, HALO, 2, 3)])
+    first = surround([(u0a, 0, 3, 3, (2, 1)), (k0, 0, 2, HALO, (3, 2))])
     gather_k = Gather(k1)
+    more = beyond(k0)
     await_all(first)
+    more += relay(k0)
 
     steps = coefficients(DEGREE)
 
@@ -430,12 +440,17 @@
         coarsen(t0, u1, mz, my, 0.125, m1)
         gather = Gather(u1)
 
-        def hold(p):
+        def hold(p, edges=True):
             for c in range(share):
                 for row in own_tiles:
                     held[p, c, pl.ds(row, TILE)] = rows_at(wb0, p, c, row)
+                if edges:
+                    for row in (PAD - 1, PAD + own_y):
+                        held[p, c, pl.ds(row, 1)] = wb0[p, c, pl.ds(row, 1)]
 
         loop(own_z, hold)
+        for p in (own_z, zs - 1):
+            hold(p, False)
         return gather
 
     def solve(u1):
@@ -475,7 +490,7 @@
                         value = value + rows_at(k1, q, c, row) * rows_at(e1, p, c // 2, row)
                         mid.put(wb1, q, c, row, value)
 
-        loop(pairs_count, add, 1)
+        loop(pairs_count, add)
 
         def near_own(reach):
             if mz + 2 * reach >= mid_planes:
@@ -510,7 +525,7 @@
                         value = rows_at(held, p, c, row) + rows_at(k0, p, c, row) * add
                         wa0[p, c, pl.ds(row, TILE)] = value
 
-        loop(mz + 2 * reach, body, 1)
+        loop(mz + 2 * reach, body)
         fine.step(u, wa0, wb0, around(3), steps[0])
         fine.step(u, wb0, wa0, around(2), steps[1])
         fine.step(u, wa0, out, around(1), steps[2], save=False, plus=plus)
@@ -525,9 +540,8 @@
 
     gather = down(u0a, ha, u1a, gather_k.forward)
     gather_k.across()
-    more = beyond(k0)
     gather.forward()
-    held = surround([(ha, HALO, HALO, 3, 3)])
+    held = surround([(ha, 1, HALO, HALO, (3, 2, 1))])
     gather_k.wait()
 
     def mid_weights(p):
@@ -541,7 +555,7 @@
         for row in low.rows:
             weigh(low, p, row)
 
-    loop(low_planes, low_weights, 4)
+    loop(low_planes, low_weights)
     gather.across()
     gather.wait()
     solve(u1a)
@@ -558,11 +572,11 @@
                 u0b[p, c, pl.ds(row, TILE)] = rows_at(m0, p, c, row) * values[c]
 
     loop(own_z, again)
-    second = surround([(u0b, 3, 3, 2, 2)])
+    second = surround([(u0b, 0, 3, 3, (2, 1))])
     await_all(second)
     gather = down(u0b, hb, u1b)
     gather.forward()
-    held = surround([(hb, HALO, HALO, 3, 3)])
+    held = surround([(hb, 1, HALO, HALO, (3, 2, 1))])
     gather.across()
     gather.wait()
     solve(u1b)
@@ -617,7 +631,7 @@
     inside = (own_z, chunks, own_y, LANES)
     vmem = lambda shape, count: [pltpu.VMEM(shape, jnp.float32)] * count
     gathers = 3 * (len(z_window) - 1 + 2 * len(pairs) - 1)
-    copies = 5 * 8 + 6 + gathers
+    copies = 5 * 4 + 4 * (3 * 2 + 2 * 3) + 6 + gathers
     return pl.pallas_call(
         functools.partial(kernel, sizes, z_window, pairs),
         out_shape=[pltpu.VMEM(source.shape, jnp.float32)] * 2,

time: 63.2 us -> 56.6 us (0.90)
  Pallas kernels: 61.2 us -> 54.2 us
    pallas_call x1, Pallas kernels: 61.2 us -> 54.2 us  [local(): pl.pallas_call(functools.partial(kernel, sizes, z_window, pairs), out_sha...]
where the time goes in v2:
time: 56.6 us; the launch traced here: 56.1 us
  Pallas kernels  54.2 us (96%)
  local copies, waits for them, and re-layouts  1.31 us (2%)
  between operations  0.64 us (1%)
    pallas_call x1, Pallas kernels, local(): pl.pallas_call(functools.partial(kernel, sizes, z_window, pairs), out_sha...  54.2 us
    unnamed x2, local copies, waits for them, and re-layouts  1.31 us

profile of v2, /device:TPU:1, one launch (start us, length us, event | category | flops | bytes accessed | tf_op | source)
XLA Modules:
  0.0 56.1 jit_solution(7252355304256436469)
XLA Ops:
  0.6 54.2 %shard_map.41 = (f32[4,16,512]{2,1,0:T(8,128)S(1)}, f32[4,16,512]{2,1,0:T(8,128)S(1)}) custom-call(f32[4,16,512]{2,1,0:T(8,128)} %source.1, f32[4,16,512]{2,1,0:T(8,128)} %conduct.1), custom_call_target="tpu_custom_call" | custom-call | tf_op jit(solution)/shard_map/pallas_call | solution.py:635
  54.8 0.7 %copy.6 = f32[4,16,512]{2,1,0:T(8,128)} copy(f32[4,16,512]{2,1,0:T(8,128)S(1)} %get-tuple-element.2) | data formatting | bytes 262144
  55.5 0.7 %copy.7 = f32[4,16,512]{2,1,0:T(8,128)} copy(f32[4,16,512]{2,1,0:T(8,128)S(1)} %get-tuple-element.3) | data formatting | bytes 262144

commit v3 on v2

--- a/solution.py
+++ b/solution.py
@@ -1,4 +1,5 @@
 import functools
+import math
 
 import jax
 import jax.numpy as jnp
@@ -190,7 +191,7 @@
            raw_f, raw_k, f0, k0, m0, g0, inv0, u0a, u0b, wa0, wb0, d0, ha, hb, ws, t0,
            k1, m1, g1, inv1, u1a, u1b, wa1, wb1, d1, t1, e0,
            k2, m2, g2, inv2, u2, wa2, wb2, d2, e1,
-           load_sem, send_sem, recv_sem):
+           tally, load_sem, send_sem, recv_sem):
     gz, gy = sizes
     own_z, own_y, nx = source.shape
     mz, my = own_z // 2, own_y // 2
@@ -296,11 +297,28 @@
             src_ref=from_ref, dst_ref=to_ref, send_sem=sent, recv_sem=got,
             device_id=device, device_id_type=MESH)
 
+    shared, amounts = [], []
+
     def send(from_ref, to_ref, device):
-        copy = copy_of(from_ref, to_ref, take("send"), take("recv"), device)
+        sent, got = shared[-1] if shared else (take("send"), take("recv"))
+        copy = copy_of(from_ref, to_ref, sent, got, device)
         copy.start()
-        unsent.append(copy)
+        if shared:
+            amounts.append(math.prod(from_ref.shape) // LANES)
+        else:
+            unsent.append(copy)
         return copy
+
+    def together(sends):
+        pair = (take("send"), take("recv"))
+        shared.append(pair)
+        amounts.clear()
+        sends()
+        shared.pop()
+        all_rows = tally.at[pl.ds(0, sum(amounts))]
+        whole = copy_of(all_rows, all_rows, *pair, at(1, 0))
+        unsent.append(whole)
+        return [whole]
 
     odd = lax.rem(me_z, 2)
     sides = [2 * odd - 1, 1 - 2 * odd]
@@ -329,6 +347,9 @@
                     held.at[planes, :, pl.ds(to_row, height)], at(0, row_side))
 
     def surround(jobs):
+        return together(lambda: send_around(jobs))
+
+    def send_around(jobs):
         copies = []
         for number, side in enumerate(sides):
             for ref, skip, depth, depth_y, corners in jobs:
@@ -415,7 +436,7 @@
 
     first = surround([(u0a, 0, 3, 3, (2, 1)), (k0, 0, 2, HALO, (3, 2))])
     gather_k = Gather(k1)
-    more = beyond(k0)
+    more = together(lambda: beyond(k0))
     await_all(first)
     more += relay(k0)
 
@@ -540,8 +561,8 @@
 
     gather = down(u0a, ha, u1a, gather_k.forward)
     gather_k.across()
+    held = surround([(ha, 1, HALO, HALO, (3, 2, 1))])
     gather.forward()
-    held = surround([(ha, 1, HALO, HALO, (3, 2, 1))])
     gather_k.wait()
 
     def mid_weights(p):
@@ -575,8 +596,8 @@
     second = surround([(u0b, 0, 3, 3, (2, 1))])
     await_all(second)
     gather = down(u0b, hb, u1b)
+    held = surround([(hb, 1, HALO, HALO, (3, 2, 1))])
     gather.forward()
-    held = surround([(hb, 1, HALO, HALO, (3, 2, 1))])
     gather.across()
     gather.wait()
     solve(u1b)
@@ -631,7 +652,7 @@
     inside = (own_z, chunks, own_y, LANES)
     vmem = lambda shape, count: [pltpu.VMEM(shape, jnp.float32)] * count
     gathers = 3 * (len(z_window) - 1 + 2 * len(pairs) - 1)
-    copies = 5 * 4 + 4 * (3 * 2 + 2 * 3) + 6 + gathers
+    copies = 6 + gathers
     return pl.pallas_call(
         functools.partial(kernel, sizes, z_window, pairs),
         out_shape=[pltpu.VMEM(source.shape, jnp.float32)] * 2,
@@ -639,6 +660,7 @@
         out_specs=[pl.BlockSpec(memory_space=pltpu.VMEM)] * 2,
         scratch_shapes=vmem(source.shape, 2) + vmem(inside, 1) + vmem(fine, 13)
         + vmem(mid, 10) + vmem(lifted, 1) + vmem(low, 8) + vmem(lifted_low, 1) + [
+            pltpu.VMEM((2 * fine[0] * chunks * own_y, LANES), jnp.float32),
             pltpu.SemaphoreType.DMA((2,)),
             pltpu.SemaphoreType.DMA((copies,)),
             pltpu.SemaphoreType.DMA((copies,)),

time: 56.6 us -> 54.3 us (0.959)
  Pallas kernels: 54.2 us -> 52.2 us
    pallas_call x1, Pallas kernels: 54.2 us -> 52.2 us  [local(): pl.pallas_call(functools.partial(kernel, sizes, z_window, pairs), out_sha...]
where the time goes in v3:
time: 54.3 us; the launch traced here: 54.1 us
  Pallas kernels  52.2 us (96%)
  local copies, waits for them, and re-layouts  1.31 us (2%)
  between operations  0.64 us (1%)
    pallas_call x1, Pallas kernels, local(): pl.pallas_call(functools.partial(kernel, sizes, z_window, pairs), out_sha...  52.2 us
    unnamed x2, local copies, waits for them, and re-layouts  1.31 us

profile of v3, /device:TPU:1, one launch (start us, length us, event | category | flops | bytes accessed | tf_op | source)
XLA Modules:
  0.0 54.1 jit_solution(15432137476949261087)
XLA Ops:
  0.6 52.2 %shard_map.41 = (f32[4,16,512]{2,1,0:T(8,128)S(1)}, f32[4,16,512]{2,1,0:T(8,128)S(1)}) custom-call(f32[4,16,512]{2,1,0:T(8,128)} %source.1, f32[4,16,512]{2,1,0:T(8,128)} %conduct.1), custom_call_target="tpu_custom_call" | custom-call | tf_op jit(solution)/shard_map/pallas_call | solution.py:656
  52.8 0.7 %copy.6 = f32[4,16,512]{2,1,0:T(8,128)} copy(f32[4,16,512]{2,1,0:T(8,128)S(1)} %get-tuple-element.2) | data formatting | bytes 262144
  53.5 0.7 %copy.7 = f32[4,16,512]{2,1,0:T(8,128)} copy(f32[4,16,512]{2,1,0:T(8,128)S(1)} %get-tuple-element.3) | data formatting | bytes 262144
